TPU v7x, 32 devices: a whole 2x2x4 slice. The times are simulated.
32 devices in a mesh: gx: 4 (over y, core), gy: 8 (over z, x).
Axes of the slice: x: 2, y: 2, z: 4, core: 2. Of those that a mesh axis runs over, the one named last changes fastest.
Arguments:
- source: float32 [64, 16, 1024], P(None, 'gx', 'gy'), may hold values from -6 to 6
- initial: float32 [64, 16, 1024], P(None, 'gx', 'gy'), may hold values from -6 to 6
- reaction: float32 [64, 16, 1024], P(None, 'gx', 'gy'), may hold values from 1 to 3
- stiffness: float32 [16, 1024], P('gx', 'gy'), may hold values from 0.5 to 2
- line_op: float32 [8, 8], replicated, may hold values from -1.6 to 5.6
- face_deriv: float32 [8], replicated, may hold values from -2 to 2
- wall_flags: int32 [4, 16, 1024], P(None, 'gx', 'gy'), may hold values 0 or 1
Outputs:
- hessenberg: float32 [6, 5], replicated
- krylov_basis: float32 [6, 64, 16, 1024], P(None, None, 'gx', 'gy')
All inputs are finite; a program needn't handle non-finite values. No bound on the sum of `wall_flags` on one device may be relied on, other than what follows from the above.
Results may differ from a plain program's by a relative error of at most 0.0003.
Values sent between devices are 32-bit elements; how exact they have to be, the bound alone decides.
A program may use at most 64 MiB of HBM per device.

v0:
```python
import jax
import jax.numpy as jnp
from jax import lax
from jax.sharding import PartitionSpec as P

P_SIZE = 8
ITERS = 5
TAU = 2.0
FLOOR = 0.1


def extended(array, sides, width):
    for axis, dim in sides:
        devices, length = (lax.axis_size(axis), array.shape[dim])
        up = [(i, (i + 1) % devices) for i in range(devices)]
        down = [(j, i) for i, j in up]
        last = lax.slice_in_dim(array, length - width, length, axis=dim)
        leading = lax.slice_in_dim(array, 0, width, axis=dim)
        before = lax.ppermute(last, axis, up)
        after = lax.ppermute(leading, axis, down)
        array = jnp.concatenate([before, array, after], axis=dim)
    return array


def local_total(values):
    return jnp.sum(jnp.sum(values, axis=0))


def x_traces(nodes, face_deriv):
    highest = lax.Precision.HIGHEST
    lower = jnp.einsum("c,cbxy->bxy", face_deriv, nodes, precision=highest)
    upper = jnp.einsum("c,cbxy->bxy", face_deriv[::-1], nodes, precision=highest)
    return jnp.stack([nodes[0], lower, nodes[-1], upper])


def y_traces(nodes, face_deriv):
    highest = lax.Precision.HIGHEST
    lower = jnp.einsum("c,acxy->axy", face_deriv, nodes, precision=highest)
    upper = jnp.einsum("c,acxy->axy", face_deriv[::-1], nodes, precision=highest)
    return jnp.stack([nodes[:, 0], lower, nodes[:, -1], upper])


def apply_op(field, reaction, stiffness, line_op, face_deriv, opened):
    highest = lax.Precision.HIGHEST
    nodes = field.reshape(P_SIZE, P_SIZE, field.shape[1], field.shape[2])
    interior = stiffness * (
        jnp.einsum("ac,cbxy->abxy", line_op, nodes, precision=highest)
        + jnp.einsum("bc,acxy->abxy", line_op, nodes, precision=highest)
    )
    padded = extended(nodes, (("gx", 2), ("gy", 3)), 1)
    xside = x_traces(padded, face_deriv)[:, :, :, 1:-1]
    yside = y_traces(padded, face_deriv)[:, :, 1:-1, :]
    x_own = xside[:, :, 1:-1]
    y_own = yside[:, :, :, 1:-1]
    east_nb = xside[0:2, :, 2:]
    west_nb = xside[2:4, :, :-2]
    north_nb = yside[0:2, :, :, 2:]
    south_nb = yside[2:4, :, :, :-2]
    add_east = TAU * (x_own[2] - opened[1] * east_nb[0]) + 0.5 * (x_own[3] - opened[1] * east_nb[1])
    add_west = TAU * (x_own[0] - opened[0] * west_nb[0]) + 0.5 * (x_own[1] - opened[0] * west_nb[1])
    add_north = TAU * (y_own[2] - opened[3] * north_nb[0]) + 0.5 * (
        y_own[3] - opened[3] * north_nb[1]
    )
    add_south = TAU * (y_own[0] - opened[2] * south_nb[0]) + 0.5 * (
        y_own[1] - opened[2] * south_nb[1]
    )
    result = reaction.reshape(nodes.shape) * nodes + interior
    result = result.at[0].add(add_west).at[P_SIZE - 1].add(add_east)
    result = result.at[:, 0].add(add_south).at[:, P_SIZE - 1].add(add_north)
    return result.reshape(field.shape)


def norm_scale(vector, total):
    squares = lax.psum(local_total(vector * vector), ("gx", "gy"))
    return jnp.sqrt(squares / total + FLOOR)


def body(source, initial, reaction, stiffness, line_op, face_deriv, wall_flags):
    highest = lax.Precision.HIGHEST
    total = float(
        P_SIZE
        * P_SIZE
        * source.shape[1]
        * lax.axis_size("gx")
        * source.shape[2]
        * lax.axis_size("gy")
    )
    opened = 1.0 - wall_flags.astype(jnp.float32)

    def operate(field):
        return apply_op(field, reaction, stiffness, line_op, face_deriv, opened)

    def products(basis, image):
        per_cell = jnp.einsum("kqxy,qxy->kxy", basis, image, precision=highest)
        return jnp.sum(per_cell, axis=(1, 2))

    first = source - operate(initial)
    basis = jnp.zeros((ITERS + 1,) + source.shape, jnp.float32)
    hessen = jnp.zeros((ITERS + 1, ITERS), jnp.float32)
    rows = lax.broadcasted_iota(jnp.int32, (ITERS + 1, ITERS), 0)
    cols = lax.broadcasted_iota(jnp.int32, (ITERS + 1, ITERS), 1)
    slots = lax.broadcasted_iota(jnp.int32, (ITERS + 1,), 0)

    def advance(step, carry):
        basis, hessen, pending = carry
        image = operate(pending)
        local = products(basis, image)
        projected, crossed, squares = lax.psum(
            (local, local_total(pending * image), local_total(pending * pending)), ("gx", "gy")
        )
        beta = jnp.sqrt(squares / total + FLOOR)
        basis = lax.dynamic_update_index_in_dim(basis, pending / beta, step, 0)
        coeffs = projected / (total * beta) + jnp.where(
            slots == step, crossed / (total * beta * beta), 0.0
        )
        pending = image / beta - jnp.einsum("k,kqxy->qxy", coeffs, basis, precision=highest)
        hessen = hessen + jnp.where(cols == step, coeffs[:, None], 0.0)
        hessen = hessen + jnp.where((rows == step) & (cols == step - 1), beta, 0.0)
        return (basis, hessen, pending)

    basis, hessen, pending = lax.fori_loop(0, ITERS, advance, (basis, hessen, first))
    beta = norm_scale(pending, total)
    basis = basis.at[ITERS].set(pending / beta)
    hessen = hessen + jnp.where((rows == ITERS) & (cols == ITERS - 1), beta, 0.0)
    return (hessen, basis)


def solution(mesh):
    return jax.shard_map(
        body,
        mesh=mesh,
        in_specs=(
            P(None, "gx", "gy"),
            P(None, "gx", "gy"),
            P(None, "gx", "gy"),
            P("gx", "gy"),
            P(),
            P(),
            P(None, "gx", "gy"),
        ),
        out_specs=(P(), P(None, None, "gx", "gy")),
        check_vma=False,
    )
```

profile of v0, /device:TPU:0, one launch (start us, length us, event | category | flops | bytes accessed | tf_op | source)
XLA Modules:
  0.0 408.1 jit_solution(16767970016116543631)
XLA Ops:
  2.2 2.0 collective-permute-start.5
  6.0 2.2 collective-permute-start.6
  8.2 3.1 collective-permute-start.7
  12.3 4.8 %collective-permute-done.6 = f32[8,8,6,1]{3,0,2,1:T(8,128)S(1)} collective-permute-done((f32[8,8,6,1]{3,0,2,1:T(8,128)S(1)}, f32[8,8,6,1]{3,0,2,1:T(8,128)S(1)}, u32[]{:S(2)}, u32[]{:S(2)}) %collective-permute-start.6) | collective-permute-done | bytes 1568 | tf_op jit(solution)/shard_map/ppermute | solution.py:19
  17.1 2.8 collective-permute-done.7
  26.0 339.5 %while.31 = (s32[]{:T(128)}, f32[6,64,4,128]{3,2,1,0:T(4,128)S(1)}, f32[6,5]{1,0:T(8,128)S(1)}, f32[64,4,128]{2,1,0:T(4,128)S(1)}, f32[64,4,128]{2,0,1:T(8,128)S...) while((s32[]{:T(128)}, f32[6,64,4,128]{3,2,1,0:T(4,128)S(1)}, ...), condition=%wide.region_6.7_spmd.clone.clone, body=%wide.region_0.6_spmd.clone.clone.sunk | while | flops 14006069 | bytes 9489035 | solution.py:121
  29.6 2.8 collective-permute-start.2
  32.7 4.3 %collective-permute-done.2 = f32[8,8,6,1]{3,0,2,1:T(8,128)S(1)} collective-permute-done((f32[8,8,6,1]{3,0,2,1:T(8,128)S(1)}, f32[8,8,6,1]{3,0,2,1:T(8,128)S(1)}, u32[]{:S(2)}, u32[]{:S(2)}) %collective-permute-start.2) | collective-permute-done | bytes 1568 | tf_op jit(solution)/shard_map/while/body/eval_jaxpr/ppermute | solution.py:20
  37.0 5.2 %collective-permute-done.3 = f32[8,8,6,1]{3,0,2,1:T(8,128)S(1)} collective-permute-done((f32[8,8,6,1]{3,0,2,1:T(8,128)S(1)}, f32[8,8,6,1]{3,0,2,1:T(8,128)S(1)}, u32[]{:S(2)}, u32[]{:S(2)}) %collective-permute-start.3) | collective-permute-done | bytes 1568 | tf_op jit(solution)/shard_map/while/body/eval_jaxpr/ppermute | solution.py:19
  47.3 2.6 convolution_bitcast_fusion.2
  49.8 39.4 %all-reduce.2 = (f32[]{:T(128)}, f32[6]{0:T(128)S(1)}, f32[]{:T(128)}) all-reduce(f32[]{:T(128)} %get-tuple-element.835, f32[6]{0:T(128)S(1)} %convolution_bitcast_fusion.2, f32[]{:T(128)} %fusion.189), channel_id=1, replica_groups=mesh['gx'=4,'gy'=8] {'gx','gy'}, use_global_device_ids=true, to_apply=%region_2.2 | all-reduce | flops 8 | bytes 64 | tf_op jit(solution)/shard_map/while/body/eval_jaxpr/psum | solution.py:108
  96.8 3.9 collective-permute-start.2
  101.0 4.9 %collective-permute-done.2 = f32[8,8,6,1]{3,0,2,1:T(8,128)S(1)} collective-permute-done((f32[8,8,6,1]{3,0,2,1:T(8,128)S(1)}, f32[8,8,6,1]{3,0,2,1:T(8,128)S(1)}, u32[]{:S(2)}, u32[]{:S(2)}) %collective-permute-start.2) | collective-permute-done | bytes 1568 | tf_op jit(solution)/shard_map/while/body/eval_jaxpr/ppermute | solution.py:20
  105.9 5.1 %collective-permute-done.3 = f32[8,8,6,1]{3,0,2,1:T(8,128)S(1)} collective-permute-done((f32[8,8,6,1]{3,0,2,1:T(8,128)S(1)}, f32[8,8,6,1]{3,0,2,1:T(8,128)S(1)}, u32[]{:S(2)}, u32[]{:S(2)}) %collective-permute-start.3) | collective-permute-done | bytes 1568 | tf_op jit(solution)/shard_map/while/body/eval_jaxpr/ppermute | solution.py:19
  116.0 2.6 convolution_bitcast_fusion.2
  118.6 39.2 %all-reduce.2 = (f32[]{:T(128)}, f32[6]{0:T(128)S(1)}, f32[]{:T(128)}) all-reduce(f32[]{:T(128)} %get-tuple-element.835, f32[6]{0:T(128)S(1)} %convolution_bitcast_fusion.2, f32[]{:T(128)} %fusion.189), channel_id=1, replica_groups=mesh['gx'=4,'gy'=8] {'gx','gy'}, use_global_device_ids=true, to_apply=%region_2.2 | all-reduce | flops 8 | bytes 64 | tf_op jit(solution)/shard_map/while/body/eval_jaxpr/psum | solution.py:108
  165.4 3.9 collective-permute-start.2
  169.6 4.6 %collective-permute-done.2 = f32[8,8,6,1]{3,0,2,1:T(8,128)S(1)} collective-permute-done((f32[8,8,6,1]{3,0,2,1:T(8,128)S(1)}, f32[8,8,6,1]{3,0,2,1:T(8,128)S(1)}, u32[]{:S(2)}, u32[]{:S(2)}) %collective-permute-start.2) | collective-permute-done | bytes 1568 | tf_op jit(solution)/shard_map/while/body/eval_jaxpr/ppermute | solution.py:20
  174.2 4.9 %collective-permute-done.3 = f32[8,8,6,1]{3,0,2,1:T(8,128)S(1)} collective-permute-done((f32[8,8,6,1]{3,0,2,1:T(8,128)S(1)}, f32[8,8,6,1]{3,0,2,1:T(8,128)S(1)}, u32[]{:S(2)}, u32[]{:S(2)}) %collective-permute-start.3) | collective-permute-done | bytes 1568 | tf_op jit(solution)/shard_map/while/body/eval_jaxpr/ppermute | solution.py:19
  184.1 2.6 convolution_bitcast_fusion.2
  186.7 39.1 %all-reduce.2 = (f32[]{:T(128)}, f32[6]{0:T(128)S(1)}, f32[]{:T(128)}) all-reduce(f32[]{:T(128)} %get-tuple-element.835, f32[6]{0:T(128)S(1)} %convolution_bitcast_fusion.2, f32[]{:T(128)} %fusion.189), channel_id=1, replica_groups=mesh['gx'=4,'gy'=8] {'gx','gy'}, use_global_device_ids=true, to_apply=%region_2.2 | all-reduce | flops 8 | bytes 64 | tf_op jit(solution)/shard_map/while/body/eval_jaxpr/psum | solution.py:108
  233.3 3.9 collective-permute-start.2
  237.6 4.6 %collective-permute-done.2 = f32[8,8,6,1]{3,0,2,1:T(8,128)S(1)} collective-permute-done((f32[8,8,6,1]{3,0,2,1:T(8,128)S(1)}, f32[8,8,6,1]{3,0,2,1:T(8,128)S(1)}, u32[]{:S(2)}, u32[]{:S(2)}) %collective-permute-start.2) | collective-permute-done | bytes 1568 | tf_op jit(solution)/shard_map/while/body/eval_jaxpr/ppermute | solution.py:20
  242.1 4.9 %collective-permute-done.3 = f32[8,8,6,1]{3,0,2,1:T(8,128)S(1)} collective-permute-done((f32[8,8,6,1]{3,0,2,1:T(8,128)S(1)}, f32[8,8,6,1]{3,0,2,1:T(8,128)S(1)}, u32[]{:S(2)}, u32[]{:S(2)}) %collective-permute-start.3) | collective-permute-done | bytes 1568 | tf_op jit(solution)/shard_map/while/body/eval_jaxpr/ppermute | solution.py:19
  252.1 2.6 convolution_bitcast_fusion.2
  254.7 39.1 %all-reduce.2 = (f32[]{:T(128)}, f32[6]{0:T(128)S(1)}, f32[]{:T(128)}) all-reduce(f32[]{:T(128)} %get-tuple-element.835, f32[6]{0:T(128)S(1)} %convolution_bitcast_fusion.2, f32[]{:T(128)} %fusion.189), channel_id=1, replica_groups=mesh['gx'=4,'gy'=8] {'gx','gy'}, use_global_device_ids=true, to_apply=%region_2.2 | all-reduce | flops 8 | bytes 64 | tf_op jit(solution)/shard_map/while/body/eval_jaxpr/psum | solution.py:108
  301.3 3.9 collective-permute-start.2
  305.5 4.6 %collective-permute-done.2 = f32[8,8,6,1]{3,0,2,1:T(8,128)S(1)} collective-permute-done((f32[8,8,6,1]{3,0,2,1:T(8,128)S(1)}, f32[8,8,6,1]{3,0,2,1:T(8,128)S(1)}, u32[]{:S(2)}, u32[]{:S(2)}) %collective-permute-start.2) | collective-permute-done | bytes 1568 | tf_op jit(solution)/shard_map/while/body/eval_jaxpr/ppermute | solution.py:20
  310.1 4.9 %collective-permute-done.3 = f32[8,8,6,1]{3,0,2,1:T(8,128)S(1)} collective-permute-done((f32[8,8,6,1]{3,0,2,1:T(8,128)S(1)}, f32[8,8,6,1]{3,0,2,1:T(8,128)S(1)}, u32[]{:S(2)}, u32[]{:S(2)}) %collective-permute-start.3) | collective-permute-done | bytes 1568 | tf_op jit(solution)/shard_map/while/body/eval_jaxpr/ppermute | solution.py:19
  320.0 2.6 convolution_bitcast_fusion.2
  322.6 39.1 %all-reduce.2 = (f32[]{:T(128)}, f32[6]{0:T(128)S(1)}, f32[]{:T(128)}) all-reduce(f32[]{:T(128)} %get-tuple-element.835, f32[6]{0:T(128)S(1)} %convolution_bitcast_fusion.2, f32[]{:T(128)} %fusion.189), channel_id=1, replica_groups=mesh['gx'=4,'gy'=8] {'gx','gy'}, use_global_device_ids=true, to_apply=%region_2.2 | all-reduce | flops 8 | bytes 64 | tf_op jit(solution)/shard_map/while/body/eval_jaxpr/psum | solution.py:108
  366.2 40.3 %psum.52 = f32[]{:T(128)} all-reduce(f32[]{:T(128)} %multiply_reduce_fusion.2), channel_id=1, replica_groups=mesh['gx'=4,'gy'=8] {'gx','gy'}, use_global_device_ids=true, to_apply=%region_8.9 | all-reduce | flops 1 | bytes 8 | tf_op jit(solution)/shard_map/psum | solution.py:74
  (322 shorter events, 68.2 us)
Async XLA Ops:
  1.5 2.6 copy-start.5
  1.6 4.1 %collective-permute-start.4 = (f32[8,8,1,128]{3,0,2,1:T(8,128)S(1)}, f32[8,8,1,128]{3,0,2,1:T(8,128)S(1)}, u32[]{:S(2)}, u32[]{:S(2)}) collective-permute-start(f32[8,8,1,128]{3,0,2,1:T(8,128)S(1)} %copy.247), channel_id=1, source_target_pairs={{0,8},{8,16},{16,24},{24,0},{1,9},{9,17},{17,25},{25,1},{2,10},{10... | collective-permute-start | bytes 98312 | tf_op jit(solution)/shard_map/ppermute | solution.py:19
  2.1 2.1 copy-start.11
  2.2 3.7 collective-permute-start.5
  5.5 6.7 %copy-start.3 = (f32[8,8,4,128]{3,0,2,1:T(8,128)}, f32[8,8,4,128]{3,0,2,1:T(8,128)S(1)}, u32[]{:S(2)}) copy-start(f32[8,8,4,128]{3,0,2,1:T(8,128)S(1)} %fusion.62) | copy-start | bytes 393220
  6.0 11.1 %collective-permute-start.6 = (f32[8,8,6,1]{3,0,2,1:T(8,128)S(1)}, f32[8,8,6,1]{3,0,2,1:T(8,128)S(1)}, u32[]{:S(2)}, u32[]{:S(2)}) collective-permute-start(f32[8,8,6,1]{3,0,2,1:T(8,128)S(1)} %get-tuple-element.682), channel_id=1, source_target_pairs={{0,1},{1,2},{2,3},{3,4},{4,5},{5,6},{6,7},{7,0},{8,9},{9,10},{10,1... | collective-permute-start | bytes 4616 | tf_op jit(solution)/shard_map/ppermute | solution.py:19
  8.2 11.6 %collective-permute-start.7 = (f32[8,8,6,1]{3,0,2,1:T(8,128)S(1)}, f32[8,8,6,1]{3,0,2,1:T(8,128)S(1)}, u32[]{:S(2)}, u32[]{:S(2)}) collective-permute-start(f32[8,8,6,1]{3,0,2,1:T(8,128)S(1)} %get-tuple-element.683), channel_id=1, source_target_pairs={{1,0},{2,1},{3,2},{4,3},{5,4},{6,5},{7,6},{0,7},{9,8},{10,9},{11,1... | collective-permute-start | bytes 4616 | tf_op jit(solution)/shard_map/ppermute | solution.py:20
  26.1 3.4 collective-permute-start
  26.3 3.2 collective-permute-start.1
  28.5 4.2 %copy-start.1 = (f32[8,8,4,128]{3,0,2,1:T(8,128)}, f32[8,8,4,128]{3,0,2,1:T(8,128)S(1)}, u32[]{:S(2)}) copy-start(f32[8,8,4,128]{3,0,2,1:T(8,128)S(1)} %fusion.175) | copy-start | bytes 393220 | tf_op jit(solution)/shard_map/while
  29.6 7.4 %collective-permute-start.2 = (f32[8,8,6,1]{3,0,2,1:T(8,128)S(1)}, f32[8,8,6,1]{3,0,2,1:T(8,128)S(1)}, u32[]{:S(2)}, u32[]{:S(2)}) collective-permute-start(f32[8,8,6,1]{3,0,2,1:T(8,128)S(1)} %get-tuple-element.788), channel_id=1, source_target_pairs={{1,0},{2,1},{3,2},{4,3},{5,4},{6,5},{7,6},{0,7},{9,8},{10,9},{11,1... | collective-permute-start | bytes 4616 | tf_op jit(solution)/shard_map/while/body/eval_jaxpr/ppermute | solution.py:20
  32.4 9.8 %collective-permute-start.3 = (f32[8,8,6,1]{3,0,2,1:T(8,128)S(1)}, f32[8,8,6,1]{3,0,2,1:T(8,128)S(1)}, u32[]{:S(2)}, u32[]{:S(2)}) collective-permute-start(f32[8,8,6,1]{3,0,2,1:T(8,128)S(1)} %get-tuple-element.789), channel_id=1, source_target_pairs={{0,1},{1,2},{2,3},{3,4},{4,5},{5,6},{6,7},{7,0},{8,9},{9,10},{10,1... | collective-permute-start | bytes 4616 | tf_op jit(solution)/shard_map/while/body/eval_jaxpr/ppermute | solution.py:19
  93.1 3.4 collective-permute-start
  93.2 3.5 collective-permute-start.1
  95.5 5.4 %copy-start.1 = (f32[8,8,4,128]{3,0,2,1:T(8,128)}, f32[8,8,4,128]{3,0,2,1:T(8,128)S(1)}, u32[]{:S(2)}) copy-start(f32[8,8,4,128]{3,0,2,1:T(8,128)S(1)} %fusion.175) | copy-start | bytes 393220 | tf_op jit(solution)/shard_map/while
  96.8 9.2 %collective-permute-start.2 = (f32[8,8,6,1]{3,0,2,1:T(8,128)S(1)}, f32[8,8,6,1]{3,0,2,1:T(8,128)S(1)}, u32[]{:S(2)}, u32[]{:S(2)}) collective-permute-start(f32[8,8,6,1]{3,0,2,1:T(8,128)S(1)} %get-tuple-element.788), channel_id=1, source_target_pairs={{1,0},{2,1},{3,2},{4,3},{5,4},{6,5},{7,6},{0,7},{9,8},{10,9},{11,1... | collective-permute-start | bytes 4616 | tf_op jit(solution)/shard_map/while/body/eval_jaxpr/ppermute | solution.py:20
  100.7 10.3 %collective-permute-start.3 = (f32[8,8,6,1]{3,0,2,1:T(8,128)S(1)}, f32[8,8,6,1]{3,0,2,1:T(8,128)S(1)}, u32[]{:S(2)}, u32[]{:S(2)}) collective-permute-start(f32[8,8,6,1]{3,0,2,1:T(8,128)S(1)} %get-tuple-element.789), channel_id=1, source_target_pairs={{0,1},{1,2},{2,3},{3,4},{4,5},{5,6},{6,7},{7,0},{8,9},{9,10},{10,1... | collective-permute-start | bytes 4616 | tf_op jit(solution)/shard_map/while/body/eval_jaxpr/ppermute | solution.py:19
  161.7 3.4 collective-permute-start
  161.8 3.5 collective-permute-start.1
  164.1 5.4 %copy-start.1 = (f32[8,8,4,128]{3,0,2,1:T(8,128)}, f32[8,8,4,128]{3,0,2,1:T(8,128)S(1)}, u32[]{:S(2)}) copy-start(f32[8,8,4,128]{3,0,2,1:T(8,128)S(1)} %fusion.175) | copy-start | bytes 393220 | tf_op jit(solution)/shard_map/while
  165.4 8.8 %collective-permute-start.2 = (f32[8,8,6,1]{3,0,2,1:T(8,128)S(1)}, f32[8,8,6,1]{3,0,2,1:T(8,128)S(1)}, u32[]{:S(2)}, u32[]{:S(2)}) collective-permute-start(f32[8,8,6,1]{3,0,2,1:T(8,128)S(1)} %get-tuple-element.788), channel_id=1, source_target_pairs={{1,0},{2,1},{3,2},{4,3},{5,4},{6,5},{7,6},{0,7},{9,8},{10,9},{11,1... | collective-permute-start | bytes 4616 | tf_op jit(solution)/shard_map/while/body/eval_jaxpr/ppermute | solution.py:20
  169.3 9.8 %collective-permute-start.3 = (f32[8,8,6,1]{3,0,2,1:T(8,128)S(1)}, f32[8,8,6,1]{3,0,2,1:T(8,128)S(1)}, u32[]{:S(2)}, u32[]{:S(2)}) collective-permute-start(f32[8,8,6,1]{3,0,2,1:T(8,128)S(1)} %get-tuple-element.789), channel_id=1, source_target_pairs={{0,1},{1,2},{2,3},{3,4},{4,5},{5,6},{6,7},{7,0},{8,9},{9,10},{10,1... | collective-permute-start | bytes 4616 | tf_op jit(solution)/shard_map/while/body/eval_jaxpr/ppermute | solution.py:19
  229.7 3.4 collective-permute-start
  229.7 3.5 collective-permute-start.1
  232.1 5.4 %copy-start.1 = (f32[8,8,4,128]{3,0,2,1:T(8,128)}, f32[8,8,4,128]{3,0,2,1:T(8,128)S(1)}, u32[]{:S(2)}) copy-start(f32[8,8,4,128]{3,0,2,1:T(8,128)S(1)} %fusion.175) | copy-start | bytes 393220 | tf_op jit(solution)/shard_map/while
  233.3 8.8 %collective-permute-start.2 = (f32[8,8,6,1]{3,0,2,1:T(8,128)S(1)}, f32[8,8,6,1]{3,0,2,1:T(8,128)S(1)}, u32[]{:S(2)}, u32[]{:S(2)}) collective-permute-start(f32[8,8,6,1]{3,0,2,1:T(8,128)S(1)} %get-tuple-element.788), channel_id=1, source_target_pairs={{1,0},{2,1},{3,2},{4,3},{5,4},{6,5},{7,6},{0,7},{9,8},{10,9},{11,1... | collective-permute-start | bytes 4616 | tf_op jit(solution)/shard_map/while/body/eval_jaxpr/ppermute | solution.py:20
  237.3 9.8 %collective-permute-start.3 = (f32[8,8,6,1]{3,0,2,1:T(8,128)S(1)}, f32[8,8,6,1]{3,0,2,1:T(8,128)S(1)}, u32[]{:S(2)}, u32[]{:S(2)}) collective-permute-start(f32[8,8,6,1]{3,0,2,1:T(8,128)S(1)} %get-tuple-element.789), channel_id=1, source_target_pairs={{0,1},{1,2},{2,3},{3,4},{4,5},{5,6},{6,7},{7,0},{8,9},{9,10},{10,1... | collective-permute-start | bytes 4616 | tf_op jit(solution)/shard_map/while/body/eval_jaxpr/ppermute | solution.py:19
  297.6 3.4 collective-permute-start
  297.7 3.5 collective-permute-start.1
  300.0 5.4 %copy-start.1 = (f32[8,8,4,128]{3,0,2,1:T(8,128)}, f32[8,8,4,128]{3,0,2,1:T(8,128)S(1)}, u32[]{:S(2)}) copy-start(f32[8,8,4,128]{3,0,2,1:T(8,128)S(1)} %fusion.175) | copy-start | bytes 393220 | tf_op jit(solution)/shard_map/while
  301.3 8.8 %collective-permute-start.2 = (f32[8,8,6,1]{3,0,2,1:T(8,128)S(1)}, f32[8,8,6,1]{3,0,2,1:T(8,128)S(1)}, u32[]{:S(2)}, u32[]{:S(2)}) collective-permute-start(f32[8,8,6,1]{3,0,2,1:T(8,128)S(1)} %get-tuple-element.788), channel_id=1, source_target_pairs={{1,0},{2,1},{3,2},{4,3},{5,4},{6,5},{7,6},{0,7},{9,8},{10,9},{11,1... | collective-permute-start | bytes 4616 | tf_op jit(solution)/shard_map/while/body/eval_jaxpr/ppermute | solution.py:20
  305.2 9.8 %collective-permute-start.3 = (f32[8,8,6,1]{3,0,2,1:T(8,128)S(1)}, f32[8,8,6,1]{3,0,2,1:T(8,128)S(1)}, u32[]{:S(2)}, u32[]{:S(2)}) collective-permute-start(f32[8,8,6,1]{3,0,2,1:T(8,128)S(1)} %get-tuple-element.789), channel_id=1, source_target_pairs={{0,1},{1,2},{2,3},{3,4},{4,5},{5,6},{6,7},{7,0},{8,9},{9,10},{10,1... | collective-permute-start | bytes 4616 | tf_op jit(solution)/shard_map/while/body/eval_jaxpr/ppermute | solution.py:19
  (18 other events, 16.1 us)
where the time goes:
time: 410 us; the launch traced here: 408 us
  blocking collectives  236 us (58%)
  waiting for transfers between devices  61.2 us (15%)
  matrix products  36.9 us (9%)
  starting transfers between devices  35.6 us (9%)
  local copies, waits for them, and re-layouts  15.6 us (4%)
  other arithmetic  13.3 us (3%)
  loops' own time  7.86 us (2%)
    psum x5, blocking collectives, advance(): lax.psum((local, local_total(pending * image), local_total(pending * pend...  196 us
    psum x1, blocking collectives, norm_scale(): squares = lax.psum(local_total(vector * vector), ('gx', 'gy'))  40.3 us
    ppermute x12, waiting for transfers between devices, extended(): before = lax.ppermute(last, axis, up)  34.7 us
    ppermute x12, starting transfers between devices, extended(): after = lax.ppermute(leading, axis, down)  32.4 us
    ppermute x12, waiting for transfers between devices, extended(): after = lax.ppermute(leading, axis, down)  26.5 us
    dot_general x5, matrix products, products(): per_cell = jnp.einsum('kqxy,qxy->kxy', basis, image, precision=highest)  13 us
    reduce_sum x12, other arithmetic, local_total(): return jnp.sum(jnp.sum(values, axis=0))  8.74 us
  transfers between devices with their start and end apart: 24, of which 23 were waited for; matrix products, arithmetic and copies ran while one was open for 1% of the time, Pallas kernels for 0%

commit v1 on v0

--- a/solution.py
+++ b/solution.py
@@ -7,6 +7,11 @@
 ITERS = 5
 TAU = 2.0
 FLOOR = 0.1
+
+
+def by_each_axis(value, axis_one, axis_two):
+    partial = lax.psum(value, axis_one)
+    return lax.psum(partial, axis_two)
 
 
 def extended(array, sides, width):
@@ -105,8 +110,8 @@
         basis, hessen, pending = carry
         image = operate(pending)
         local = products(basis, image)
-        projected, crossed, squares = lax.psum(
-            (local, local_total(pending * image), local_total(pending * pending)), ("gx", "gy")
+        projected, crossed, squares = by_each_axis(
+            (local, local_total(pending * image), local_total(pending * pending)), "gy", "gx"
         )
         beta = jnp.sqrt(squares / total + FLOOR)
         basis = lax.dynamic_update_index_in_dim(basis, pending / beta, step, 0)

time: 410 us -> 332 us (0.81)
  blocking collectives: 236 us -> 167 us
  starting transfers between devices: 35.6 us -> 28.2 us
    psum x5 -> x10, blocking collectives: 196 us -> 130 us  [the longest x5 98.4 us: by_each_axis(): partial = lax.psum(value, axis_one)]
    ppermute x12, waiting for transfers between devices: 34.7 us -> 19.4 us  [extended(): before = lax.ppermute(last, axis, up)]
    ppermute x12, waiting for transfers between devices: 26.5 us -> 41 us  [extended(): after = lax.ppermute(leading, axis, down)]
    ppermute x12, starting transfers between devices: 32.4 us -> 19.5 us  [extended(): after = lax.ppermute(leading, axis, down)]
    ppermute x12, starting transfers between devices: 3.28 us -> 8.7 us  [extended(): before = lax.ppermute(last, axis, up)]
  transfers between devices with their start and end apart: 24 -> 24, of which waited for: 23 -> 16; matrix products, arithmetic and copies ran while one was open for 1% -> 2% of each run, Pallas kernels for 0% -> 0%
where the time goes in v1:
time: 332 us; the launch traced here: 331 us
  blocking collectives  167 us (50%)
  waiting for transfers between devices  60.4 us (18%)
  matrix products  37 us (11%)
  starting transfers between devices  28.2 us (8%)
  local copies, waits for them, and re-layouts  15.6 us (5%)
  other arithmetic  13.2 us (4%)
  loops' own time  7.86 us (2%)
    psum x5, blocking collectives, by_each_axis(): partial = lax.psum(value, axis_one)  98.4 us
    ppermute x12, waiting for transfers between devices, extended(): after = lax.ppermute(leading, axis, down)  41 us
    psum x1, blocking collectives, norm_scale(): squares = lax.psum(local_total(vector * vector), ('gx', 'gy'))  37 us
    psum x5, blocking collectives, by_each_axis(): return lax.psum(partial, axis_two)  31.7 us
    ppermute x12, starting transfers between devices, extended(): after = lax.ppermute(leading, axis, down)  19.5 us
    ppermute x12, waiting for transfers between devices, extended(): before = lax.ppermute(last, axis, up)  19.4 us
    dot_general x5, matrix products, products(): per_cell = jnp.einsum('kqxy,qxy->kxy', basis, image, precision=highest)  13 us
    ppermute x12, starting transfers between devices, extended(): before = lax.ppermute(last, axis, up)  8.7 us
  transfers between devices with their start and end apart: 24, of which 16 were waited for; matrix products, arithmetic and copies ran while one was open for 2% of the time, Pallas kernels for 0%

profile of v1, /device:TPU:0, one launch (start us, length us, event | category | flops | bytes accessed | tf_op | source)
XLA Modules:
  0.0 330.9 jit_solution(3461295096444661622)
XLA Ops:
  2.2 2.0 collective-permute-start.5
  6.0 2.2 collective-permute-start.6
  8.2 3.1 collective-permute-start.7
  12.3 4.8 %collective-permute-done.6 = f32[8,8,6,1]{3,0,2,1:T(8,128)S(1)} collective-permute-done((f32[8,8,6,1]{3,0,2,1:T(8,128)S(1)}, f32[8,8,6,1]{3,0,2,1:T(8,128)S(1)}, u32[]{:S(2)}, u32[]{:S(2)}) %collective-permute-start.6) | collective-permute-done | bytes 1568 | tf_op jit(solution)/shard_map/ppermute | solution.py:24
  17.1 2.8 collective-permute-done.7
  26.0 265.6 %while.31 = (s32[]{:T(128)}, f32[6,64,4,128]{3,2,1,0:T(4,128)S(1)}, f32[6,5]{1,0:T(8,128)S(1)}, f32[64,4,128]{2,1,0:T(4,128)S(1)}, f32[64,4,128]{2,0,1:T(8,128)S...) while((s32[]{:T(128)}, f32[6,64,4,128]{3,2,1,0:T(4,128)S(1)}, ...), condition=%wide.region_9.10_spmd.clone.clone, body=%wide.region_0.9_spmd.clone.clone.sunk | while | flops 14006077 | bytes 9489099 | solution.py:126
  29.6 2.8 collective-permute-start.2
  32.7 4.3 %collective-permute-done.2 = f32[8,8,6,1]{3,0,2,1:T(8,128)S(1)} collective-permute-done((f32[8,8,6,1]{3,0,2,1:T(8,128)S(1)}, f32[8,8,6,1]{3,0,2,1:T(8,128)S(1)}, u32[]{:S(2)}, u32[]{:S(2)}) %collective-permute-start.2) | collective-permute-done | bytes 1568 | tf_op jit(solution)/shard_map/while/body/eval_jaxpr/ppermute | solution.py:25
  37.0 5.2 %collective-permute-done.3 = f32[8,8,6,1]{3,0,2,1:T(8,128)S(1)} collective-permute-done((f32[8,8,6,1]{3,0,2,1:T(8,128)S(1)}, f32[8,8,6,1]{3,0,2,1:T(8,128)S(1)}, u32[]{:S(2)}, u32[]{:S(2)}) %collective-permute-start.3) | collective-permute-done | bytes 1568 | tf_op jit(solution)/shard_map/while/body/eval_jaxpr/ppermute | solution.py:24
  47.2 2.6 convolution_bitcast_fusion.2
  49.8 22.0 %all-reduce.4 = (f32[]{:T(128)}, f32[6]{0:T(128)S(1)}, f32[]{:T(128)}) all-reduce(f32[]{:T(128)} %get-tuple-element.844, f32[6]{0:T(128)S(1)} %convolution_bitcast_fusion.2, f32[]{:T(128)} %fusion.189), channel_id=1, replica_groups=mesh['gx'=4,'gy'=8] {'gy'}, use_global_device_ids=true, to_apply=%region_2.2 | all-reduce | flops 8 | bytes 64 | tf_op jit(solution)/shard_map/while/body/eval_jaxpr/psum | solution.py:13
  71.8 6.3 %all-reduce.5 = (f32[]{:T(128)}, f32[6]{0:T(128)S(1)}, f32[]{:T(128)}) all-reduce(f32[]{:T(128)} %get-tuple-element.810, f32[6]{0:T(128)S(1)} %get-tuple-element.811, f32[]{:T(128)} %get-tuple-element.812), channel_id=1, replica_groups=mesh['gx'=4,'gy'=8] {'gx'}, use_global_device_ids=true, to_apply=%region_3.3 | all-reduce | flops 8 | bytes 64 | tf_op jit(solution)/shard_map/while/body/eval_jaxpr/psum | solution.py:14
  85.7 2.0 collective-permute-start.3
  87.9 9.6 %collective-permute-done.2 = f32[8,8,6,1]{3,0,2,1:T(8,128)S(1)} collective-permute-done((f32[8,8,6,1]{3,0,2,1:T(8,128)S(1)}, f32[8,8,6,1]{3,0,2,1:T(8,128)S(1)}, u32[]{:S(2)}, u32[]{:S(2)}) %collective-permute-start.2) | collective-permute-done | bytes 1568 | tf_op jit(solution)/shard_map/while/body/eval_jaxpr/ppermute | solution.py:25
  102.6 2.6 convolution_bitcast_fusion.2
  105.2 18.0 %all-reduce.4 = (f32[]{:T(128)}, f32[6]{0:T(128)S(1)}, f32[]{:T(128)}) all-reduce(f32[]{:T(128)} %get-tuple-element.844, f32[6]{0:T(128)S(1)} %convolution_bitcast_fusion.2, f32[]{:T(128)} %fusion.189), channel_id=1, replica_groups=mesh['gx'=4,'gy'=8] {'gy'}, use_global_device_ids=true, to_apply=%region_2.2 | all-reduce | flops 8 | bytes 64 | tf_op jit(solution)/shard_map/while/body/eval_jaxpr/psum | solution.py:13
  123.1 6.3 %all-reduce.5 = (f32[]{:T(128)}, f32[6]{0:T(128)S(1)}, f32[]{:T(128)}) all-reduce(f32[]{:T(128)} %get-tuple-element.810, f32[6]{0:T(128)S(1)} %get-tuple-element.811, f32[]{:T(128)} %get-tuple-element.812), channel_id=1, replica_groups=mesh['gx'=4,'gy'=8] {'gx'}, use_global_device_ids=true, to_apply=%region_3.3 | all-reduce | flops 8 | bytes 64 | tf_op jit(solution)/shard_map/while/body/eval_jaxpr/psum | solution.py:14
  136.9 1.9 collective-permute-start.2
  139.3 5.3 %collective-permute-done.2 = f32[8,8,6,1]{3,0,2,1:T(8,128)S(1)} collective-permute-done((f32[8,8,6,1]{3,0,2,1:T(8,128)S(1)}, f32[8,8,6,1]{3,0,2,1:T(8,128)S(1)}, u32[]{:S(2)}, u32[]{:S(2)}) %collective-permute-start.2) | collective-permute-done | bytes 1568 | tf_op jit(solution)/shard_map/while/body/eval_jaxpr/ppermute | solution.py:25
  144.5 4.5 %collective-permute-done.3 = f32[8,8,6,1]{3,0,2,1:T(8,128)S(1)} collective-permute-done((f32[8,8,6,1]{3,0,2,1:T(8,128)S(1)}, f32[8,8,6,1]{3,0,2,1:T(8,128)S(1)}, u32[]{:S(2)}, u32[]{:S(2)}) %collective-permute-start.3) | collective-permute-done | bytes 1568 | tf_op jit(solution)/shard_map/while/body/eval_jaxpr/ppermute | solution.py:24
  154.1 2.6 convolution_bitcast_fusion.2
  156.6 19.7 %all-reduce.4 = (f32[]{:T(128)}, f32[6]{0:T(128)S(1)}, f32[]{:T(128)}) all-reduce(f32[]{:T(128)} %get-tuple-element.844, f32[6]{0:T(128)S(1)} %convolution_bitcast_fusion.2, f32[]{:T(128)} %fusion.189), channel_id=1, replica_groups=mesh['gx'=4,'gy'=8] {'gy'}, use_global_device_ids=true, to_apply=%region_2.2 | all-reduce | flops 8 | bytes 64 | tf_op jit(solution)/shard_map/while/body/eval_jaxpr/psum | solution.py:13
  176.3 6.3 %all-reduce.5 = (f32[]{:T(128)}, f32[6]{0:T(128)S(1)}, f32[]{:T(128)}) all-reduce(f32[]{:T(128)} %get-tuple-element.810, f32[6]{0:T(128)S(1)} %get-tuple-element.811, f32[]{:T(128)} %get-tuple-element.812), channel_id=1, replica_groups=mesh['gx'=4,'gy'=8] {'gx'}, use_global_device_ids=true, to_apply=%region_3.3 | all-reduce | flops 8 | bytes 64 | tf_op jit(solution)/shard_map/while/body/eval_jaxpr/psum | solution.py:14
  192.4 9.4 %collective-permute-done.2 = f32[8,8,6,1]{3,0,2,1:T(8,128)S(1)} collective-permute-done((f32[8,8,6,1]{3,0,2,1:T(8,128)S(1)}, f32[8,8,6,1]{3,0,2,1:T(8,128)S(1)}, u32[]{:S(2)}, u32[]{:S(2)}) %collective-permute-start.2) | collective-permute-done | bytes 1568 | tf_op jit(solution)/shard_map/while/body/eval_jaxpr/ppermute | solution.py:25
  206.9 2.6 convolution_bitcast_fusion.2
  209.5 19.1 %all-reduce.4 = (f32[]{:T(128)}, f32[6]{0:T(128)S(1)}, f32[]{:T(128)}) all-reduce(f32[]{:T(128)} %get-tuple-element.844, f32[6]{0:T(128)S(1)} %convolution_bitcast_fusion.2, f32[]{:T(128)} %fusion.189), channel_id=1, replica_groups=mesh['gx'=4,'gy'=8] {'gy'}, use_global_device_ids=true, to_apply=%region_2.2 | all-reduce | flops 8 | bytes 64 | tf_op jit(solution)/shard_map/while/body/eval_jaxpr/psum | solution.py:13
  228.6 6.3 %all-reduce.5 = (f32[]{:T(128)}, f32[6]{0:T(128)S(1)}, f32[]{:T(128)}) all-reduce(f32[]{:T(128)} %get-tuple-element.810, f32[6]{0:T(128)S(1)} %get-tuple-element.811, f32[]{:T(128)} %get-tuple-element.812), channel_id=1, replica_groups=mesh['gx'=4,'gy'=8] {'gx'}, use_global_device_ids=true, to_apply=%region_3.3 | all-reduce | flops 8 | bytes 64 | tf_op jit(solution)/shard_map/while/body/eval_jaxpr/psum | solution.py:14
  244.7 9.4 %collective-permute-done.2 = f32[8,8,6,1]{3,0,2,1:T(8,128)S(1)} collective-permute-done((f32[8,8,6,1]{3,0,2,1:T(8,128)S(1)}, f32[8,8,6,1]{3,0,2,1:T(8,128)S(1)}, u32[]{:S(2)}, u32[]{:S(2)}) %collective-permute-start.2) | collective-permute-done | bytes 1568 | tf_op jit(solution)/shard_map/while/body/eval_jaxpr/ppermute | solution.py:25
  259.1 2.6 convolution_bitcast_fusion.2
  261.7 19.6 %all-reduce.4 = (f32[]{:T(128)}, f32[6]{0:T(128)S(1)}, f32[]{:T(128)}) all-reduce(f32[]{:T(128)} %get-tuple-element.844, f32[6]{0:T(128)S(1)} %convolution_bitcast_fusion.2, f32[]{:T(128)} %fusion.189), channel_id=1, replica_groups=mesh['gx'=4,'gy'=8] {'gy'}, use_global_device_ids=true, to_apply=%region_2.2 | all-reduce | flops 8 | bytes 64 | tf_op jit(solution)/shard_map/while/body/eval_jaxpr/psum | solution.py:13
  281.4 6.3 %all-reduce.5 = (f32[]{:T(128)}, f32[6]{0:T(128)S(1)}, f32[]{:T(128)}) all-reduce(f32[]{:T(128)} %get-tuple-element.810, f32[6]{0:T(128)S(1)} %get-tuple-element.811, f32[]{:T(128)} %get-tuple-element.812), channel_id=1, replica_groups=mesh['gx'=4,'gy'=8] {'gx'}, use_global_device_ids=true, to_apply=%region_3.3 | all-reduce | flops 8 | bytes 64 | tf_op jit(solution)/shard_map/while/body/eval_jaxpr/psum | solution.py:14
  292.2 37.0 %psum.97 = f32[]{:T(128)} all-reduce(f32[]{:T(128)} %multiply_reduce_fusion.2), channel_id=1, replica_groups=mesh['gx'=4,'gy'=8] {'gx','gy'}, use_global_device_ids=true, to_apply=%region_11.12 | all-reduce | flops 1 | bytes 8 | tf_op jit(solution)/shard_map/psum | solution.py:79
  (327 shorter events, 72.1 us)
Async XLA Ops:
  1.5 2.6 copy-start.5
  1.6 4.1 %collective-permute-start.4 = (f32[8,8,1,128]{3,0,2,1:T(8,128)S(1)}, f32[8,8,1,128]{3,0,2,1:T(8,128)S(1)}, u32[]{:S(2)}, u32[]{:S(2)}) collective-permute-start(f32[8,8,1,128]{3,0,2,1:T(8,128)S(1)} %copy.247), channel_id=1, source_target_pairs={{0,8},{8,16},{16,24},{24,0},{1,9},{9,17},{17,25},{25,1},{2,10},{10... | collective-permute-start | bytes 98312 | tf_op jit(solution)/shard_map/ppermute | solution.py:24
  2.1 2.1 copy-start.11
  2.2 3.7 %collective-permute-start.5 = (f32[8,8,1,128]{3,0,2,1:T(8,128)S(1)}, f32[8,8,1,128]{3,0,2,1:T(8,128)S(1)}, u32[]{:S(2)}, u32[]{:S(2)}) collective-permute-start(f32[8,8,1,128]{3,0,2,1:T(8,128)S(1)} %copy.248), channel_id=1, source_target_pairs={{8,0},{16,8},{24,16},{0,24},{9,1},{17,9},{25,17},{1,25},{10,2},{18... | collective-permute-start | bytes 98312 | tf_op jit(solution)/shard_map/ppermute | solution.py:25
  5.5 6.7 %copy-start.3 = (f32[8,8,4,128]{3,0,2,1:T(8,128)}, f32[8,8,4,128]{3,0,2,1:T(8,128)S(1)}, u32[]{:S(2)}) copy-start(f32[8,8,4,128]{3,0,2,1:T(8,128)S(1)} %fusion.62) | copy-start | bytes 393220
  6.0 11.1 %collective-permute-start.6 = (f32[8,8,6,1]{3,0,2,1:T(8,128)S(1)}, f32[8,8,6,1]{3,0,2,1:T(8,128)S(1)}, u32[]{:S(2)}, u32[]{:S(2)}) collective-permute-start(f32[8,8,6,1]{3,0,2,1:T(8,128)S(1)} %get-tuple-element.685), channel_id=1, source_target_pairs={{0,1},{1,2},{2,3},{3,4},{4,5},{5,6},{6,7},{7,0},{8,9},{9,10},{10,1... | collective-permute-start | bytes 4616 | tf_op jit(solution)/shard_map/ppermute | solution.py:24
  8.2 11.6 %collective-permute-start.7 = (f32[8,8,6,1]{3,0,2,1:T(8,128)S(1)}, f32[8,8,6,1]{3,0,2,1:T(8,128)S(1)}, u32[]{:S(2)}, u32[]{:S(2)}) collective-permute-start(f32[8,8,6,1]{3,0,2,1:T(8,128)S(1)} %get-tuple-element.686), channel_id=1, source_target_pairs={{1,0},{2,1},{3,2},{4,3},{5,4},{6,5},{7,6},{0,7},{9,8},{10,9},{11,1... | collective-permute-start | bytes 4616 | tf_op jit(solution)/shard_map/ppermute | solution.py:25
  26.0 3.4 %collective-permute-start = (f32[8,8,1,128]{3,0,2,1:T(8,128)S(1)}, f32[8,8,1,128]{3,0,2,1:T(8,128)S(1)}, u32[]{:S(2)}, u32[]{:S(2)}) collective-permute-start(f32[8,8,1,128]{3,0,2,1:T(8,128)S(1)} %copy.311), channel_id=1, source_target_pairs={{0,8},{8,16},{16,24},{24,0},{1,9},{9,17},{17,25},{25,1},{2,10},{10... | collective-permute-start | bytes 98312 | tf_op jit(solution)/shard_map/while/body/eval_jaxpr/ppermute | solution.py:24
  26.3 3.2 collective-permute-start.1
  28.5 4.2 %copy-start.1 = (f32[8,8,4,128]{3,0,2,1:T(8,128)}, f32[8,8,4,128]{3,0,2,1:T(8,128)S(1)}, u32[]{:S(2)}) copy-start(f32[8,8,4,128]{3,0,2,1:T(8,128)S(1)} %fusion.175) | copy-start | bytes 393220 | tf_op jit(solution)/shard_map/while
  29.6 7.4 %collective-permute-start.2 = (f32[8,8,6,1]{3,0,2,1:T(8,128)S(1)}, f32[8,8,6,1]{3,0,2,1:T(8,128)S(1)}, u32[]{:S(2)}, u32[]{:S(2)}) collective-permute-start(f32[8,8,6,1]{3,0,2,1:T(8,128)S(1)} %get-tuple-element.794), channel_id=1, source_target_pairs={{1,0},{2,1},{3,2},{4,3},{5,4},{6,5},{7,6},{0,7},{9,8},{10,9},{11,1... | collective-permute-start | bytes 4616 | tf_op jit(solution)/shard_map/while/body/eval_jaxpr/ppermute | solution.py:25
  32.4 9.8 %collective-permute-start.3 = (f32[8,8,6,1]{3,0,2,1:T(8,128)S(1)}, f32[8,8,6,1]{3,0,2,1:T(8,128)S(1)}, u32[]{:S(2)}, u32[]{:S(2)}) collective-permute-start(f32[8,8,6,1]{3,0,2,1:T(8,128)S(1)} %get-tuple-element.795), channel_id=1, source_target_pairs={{0,1},{1,2},{2,3},{3,4},{4,5},{5,6},{6,7},{7,0},{8,9},{9,10},{10,1... | collective-permute-start | bytes 4616 | tf_op jit(solution)/shard_map/while/body/eval_jaxpr/ppermute | solution.py:24
  82.0 3.4 %collective-permute-start = (f32[8,8,1,128]{3,0,2,1:T(8,128)S(1)}, f32[8,8,1,128]{3,0,2,1:T(8,128)S(1)}, u32[]{:S(2)}, u32[]{:S(2)}) collective-permute-start(f32[8,8,1,128]{3,0,2,1:T(8,128)S(1)} %copy.311), channel_id=1, source_target_pairs={{0,8},{8,16},{16,24},{24,0},{1,9},{9,17},{17,25},{25,1},{2,10},{10... | collective-permute-start | bytes 98312 | tf_op jit(solution)/shard_map/while/body/eval_jaxpr/ppermute | solution.py:24
  82.1 3.4 %collective-permute-start.1 = (f32[8,8,1,128]{3,0,2,1:T(8,128)S(1)}, f32[8,8,1,128]{3,0,2,1:T(8,128)S(1)}, u32[]{:S(2)}, u32[]{:S(2)}) collective-permute-start(f32[8,8,1,128]{3,0,2,1:T(8,128)S(1)} %copy.313), channel_id=1, source_target_pairs={{8,0},{16,8},{24,16},{0,24},{9,1},{17,9},{25,17},{1,25},{10,2},{18... | collective-permute-start | bytes 98312 | tf_op jit(solution)/shard_map/while/body/eval_jaxpr/ppermute | solution.py:25
  84.4 3.4 %copy-start.1 = (f32[8,8,4,128]{3,0,2,1:T(8,128)}, f32[8,8,4,128]{3,0,2,1:T(8,128)S(1)}, u32[]{:S(2)}) copy-start(f32[8,8,4,128]{3,0,2,1:T(8,128)S(1)} %fusion.175) | copy-start | bytes 393220 | tf_op jit(solution)/shard_map/while
  85.6 11.9 %collective-permute-start.2 = (f32[8,8,6,1]{3,0,2,1:T(8,128)S(1)}, f32[8,8,6,1]{3,0,2,1:T(8,128)S(1)}, u32[]{:S(2)}, u32[]{:S(2)}) collective-permute-start(f32[8,8,6,1]{3,0,2,1:T(8,128)S(1)} %get-tuple-element.794), channel_id=1, source_target_pairs={{1,0},{2,1},{3,2},{4,3},{5,4},{6,5},{7,6},{0,7},{9,8},{10,9},{11,1... | collective-permute-start | bytes 4616 | tf_op jit(solution)/shard_map/while/body/eval_jaxpr/ppermute | solution.py:25
  85.7 11.9 %collective-permute-start.3 = (f32[8,8,6,1]{3,0,2,1:T(8,128)S(1)}, f32[8,8,6,1]{3,0,2,1:T(8,128)S(1)}, u32[]{:S(2)}, u32[]{:S(2)}) collective-permute-start(f32[8,8,6,1]{3,0,2,1:T(8,128)S(1)} %get-tuple-element.795), channel_id=1, source_target_pairs={{0,1},{1,2},{2,3},{3,4},{4,5},{5,6},{6,7},{7,0},{8,9},{9,10},{10,1... | collective-permute-start | bytes 4616 | tf_op jit(solution)/shard_map/while/body/eval_jaxpr/ppermute | solution.py:24
  133.3 3.4 %collective-permute-start = (f32[8,8,1,128]{3,0,2,1:T(8,128)S(1)}, f32[8,8,1,128]{3,0,2,1:T(8,128)S(1)}, u32[]{:S(2)}, u32[]{:S(2)}) collective-permute-start(f32[8,8,1,128]{3,0,2,1:T(8,128)S(1)} %copy.311), channel_id=1, source_target_pairs={{0,8},{8,16},{16,24},{24,0},{1,9},{9,17},{17,25},{25,1},{2,10},{10... | collective-permute-start | bytes 98312 | tf_op jit(solution)/shard_map/while/body/eval_jaxpr/ppermute | solution.py:24
  133.4 3.4 %collective-permute-start.1 = (f32[8,8,1,128]{3,0,2,1:T(8,128)S(1)}, f32[8,8,1,128]{3,0,2,1:T(8,128)S(1)}, u32[]{:S(2)}, u32[]{:S(2)}) collective-permute-start(f32[8,8,1,128]{3,0,2,1:T(8,128)S(1)} %copy.313), channel_id=1, source_target_pairs={{8,0},{16,8},{24,16},{0,24},{9,1},{17,9},{25,17},{1,25},{10,2},{18... | collective-permute-start | bytes 98312 | tf_op jit(solution)/shard_map/while/body/eval_jaxpr/ppermute | solution.py:25
  135.8 3.4 %copy-start.1 = (f32[8,8,4,128]{3,0,2,1:T(8,128)}, f32[8,8,4,128]{3,0,2,1:T(8,128)S(1)}, u32[]{:S(2)}) copy-start(f32[8,8,4,128]{3,0,2,1:T(8,128)S(1)} %fusion.175) | copy-start | bytes 393220 | tf_op jit(solution)/shard_map/while
  136.9 7.6 %collective-permute-start.2 = (f32[8,8,6,1]{3,0,2,1:T(8,128)S(1)}, f32[8,8,6,1]{3,0,2,1:T(8,128)S(1)}, u32[]{:S(2)}, u32[]{:S(2)}) collective-permute-start(f32[8,8,6,1]{3,0,2,1:T(8,128)S(1)} %get-tuple-element.794), channel_id=1, source_target_pairs={{1,0},{2,1},{3,2},{4,3},{5,4},{6,5},{7,6},{0,7},{9,8},{10,9},{11,1... | collective-permute-start | bytes 4616 | tf_op jit(solution)/shard_map/while/body/eval_jaxpr/ppermute | solution.py:25
  138.8 10.2 %collective-permute-start.3 = (f32[8,8,6,1]{3,0,2,1:T(8,128)S(1)}, f32[8,8,6,1]{3,0,2,1:T(8,128)S(1)}, u32[]{:S(2)}, u32[]{:S(2)}) collective-permute-start(f32[8,8,6,1]{3,0,2,1:T(8,128)S(1)} %get-tuple-element.795), channel_id=1, source_target_pairs={{0,1},{1,2},{2,3},{3,4},{4,5},{5,6},{6,7},{7,0},{8,9},{9,10},{10,1... | collective-permute-start | bytes 4616 | tf_op jit(solution)/shard_map/while/body/eval_jaxpr/ppermute | solution.py:24
  186.5 3.4 %collective-permute-start = (f32[8,8,1,128]{3,0,2,1:T(8,128)S(1)}, f32[8,8,1,128]{3,0,2,1:T(8,128)S(1)}, u32[]{:S(2)}, u32[]{:S(2)}) collective-permute-start(f32[8,8,1,128]{3,0,2,1:T(8,128)S(1)} %copy.311), channel_id=1, source_target_pairs={{0,8},{8,16},{16,24},{24,0},{1,9},{9,17},{17,25},{25,1},{2,10},{10... | collective-permute-start | bytes 98312 | tf_op jit(solution)/shard_map/while/body/eval_jaxpr/ppermute | solution.py:24
  186.6 3.4 %collective-permute-start.1 = (f32[8,8,1,128]{3,0,2,1:T(8,128)S(1)}, f32[8,8,1,128]{3,0,2,1:T(8,128)S(1)}, u32[]{:S(2)}, u32[]{:S(2)}) collective-permute-start(f32[8,8,1,128]{3,0,2,1:T(8,128)S(1)} %copy.313), channel_id=1, source_target_pairs={{8,0},{16,8},{24,16},{0,24},{9,1},{17,9},{25,17},{1,25},{10,2},{18... | collective-permute-start | bytes 98312 | tf_op jit(solution)/shard_map/while/body/eval_jaxpr/ppermute | solution.py:25
  188.9 3.4 %copy-start.1 = (f32[8,8,4,128]{3,0,2,1:T(8,128)}, f32[8,8,4,128]{3,0,2,1:T(8,128)S(1)}, u32[]{:S(2)}) copy-start(f32[8,8,4,128]{3,0,2,1:T(8,128)S(1)} %fusion.175) | copy-start | bytes 393220 | tf_op jit(solution)/shard_map/while
  190.1 11.7 %collective-permute-start.2 = (f32[8,8,6,1]{3,0,2,1:T(8,128)S(1)}, f32[8,8,6,1]{3,0,2,1:T(8,128)S(1)}, u32[]{:S(2)}, u32[]{:S(2)}) collective-permute-start(f32[8,8,6,1]{3,0,2,1:T(8,128)S(1)} %get-tuple-element.794), channel_id=1, source_target_pairs={{1,0},{2,1},{3,2},{4,3},{5,4},{6,5},{7,6},{0,7},{9,8},{10,9},{11,1... | collective-permute-start | bytes 4616 | tf_op jit(solution)/shard_map/while/body/eval_jaxpr/ppermute | solution.py:25
  190.3 11.5 %collective-permute-start.3 = (f32[8,8,6,1]{3,0,2,1:T(8,128)S(1)}, f32[8,8,6,1]{3,0,2,1:T(8,128)S(1)}, u32[]{:S(2)}, u32[]{:S(2)}) collective-permute-start(f32[8,8,6,1]{3,0,2,1:T(8,128)S(1)} %get-tuple-element.795), channel_id=1, source_target_pairs={{0,1},{1,2},{2,3},{3,4},{4,5},{5,6},{6,7},{7,0},{8,9},{9,10},{10,1... | collective-permute-start | bytes 4616 | tf_op jit(solution)/shard_map/while/body/eval_jaxpr/ppermute | solution.py:24
  238.8 3.4 %collective-permute-start = (f32[8,8,1,128]{3,0,2,1:T(8,128)S(1)}, f32[8,8,1,128]{3,0,2,1:T(8,128)S(1)}, u32[]{:S(2)}, u32[]{:S(2)}) collective-permute-start(f32[8,8,1,128]{3,0,2,1:T(8,128)S(1)} %copy.311), channel_id=1, source_target_pairs={{0,8},{8,16},{16,24},{24,0},{1,9},{9,17},{17,25},{25,1},{2,10},{10... | collective-permute-start | bytes 98312 | tf_op jit(solution)/shard_map/while/body/eval_jaxpr/ppermute | solution.py:24
  238.9 3.4 %collective-permute-start.1 = (f32[8,8,1,128]{3,0,2,1:T(8,128)S(1)}, f32[8,8,1,128]{3,0,2,1:T(8,128)S(1)}, u32[]{:S(2)}, u32[]{:S(2)}) collective-permute-start(f32[8,8,1,128]{3,0,2,1:T(8,128)S(1)} %copy.313), channel_id=1, source_target_pairs={{8,0},{16,8},{24,16},{0,24},{9,1},{17,9},{25,17},{1,25},{10,2},{18... | collective-permute-start | bytes 98312 | tf_op jit(solution)/shard_map/while/body/eval_jaxpr/ppermute | solution.py:25
  241.2 3.4 %copy-start.1 = (f32[8,8,4,128]{3,0,2,1:T(8,128)}, f32[8,8,4,128]{3,0,2,1:T(8,128)S(1)}, u32[]{:S(2)}) copy-start(f32[8,8,4,128]{3,0,2,1:T(8,128)S(1)} %fusion.175) | copy-start | bytes 393220 | tf_op jit(solution)/shard_map/while
  242.4 11.7 %collective-permute-start.2 = (f32[8,8,6,1]{3,0,2,1:T(8,128)S(1)}, f32[8,8,6,1]{3,0,2,1:T(8,128)S(1)}, u32[]{:S(2)}, u32[]{:S(2)}) collective-permute-start(f32[8,8,6,1]{3,0,2,1:T(8,128)S(1)} %get-tuple-element.794), channel_id=1, source_target_pairs={{1,0},{2,1},{3,2},{4,3},{5,4},{6,5},{7,6},{0,7},{9,8},{10,9},{11,1... | collective-permute-start | bytes 4616 | tf_op jit(solution)/shard_map/while/body/eval_jaxpr/ppermute | solution.py:25
  243.1 11.0 %collective-permute-start.3 = (f32[8,8,6,1]{3,0,2,1:T(8,128)S(1)}, f32[8,8,6,1]{3,0,2,1:T(8,128)S(1)}, u32[]{:S(2)}, u32[]{:S(2)}) collective-permute-start(f32[8,8,6,1]{3,0,2,1:T(8,128)S(1)} %get-tuple-element.795), channel_id=1, source_target_pairs={{0,1},{1,2},{2,3},{3,4},{4,5},{5,6},{6,7},{7,0},{8,9},{9,10},{10,1... | collective-permute-start | bytes 4616 | tf_op jit(solution)/shard_map/while/body/eval_jaxpr/ppermute | solution.py:24
  (18 other events, 16.1 us)
